TPU v7x, 256 devices: a 4x2x16 block of a 4x16x16 slice. The times are simulated.
256 devices in a mesh: groups: 2 (over y), blk: 16 (over z), ulysses: 4 (over x), cfg: 2 (over core).
Axes of the slice: x: 4, y: 2, z: 16, core: 2. Of those that a mesh axis runs over, the one named last changes fastest.
The devices are a block of a 4x16x16 slice.
Arguments:
- img_tokens: bfloat16 [2, 2, 4096, 2432], P('cfg', 'groups', ('blk', 'ulysses')), parts along dimension 1, may hold values from -72 to 72
- text_tokens: bfloat16 [2, 2, 384, 2432], P('cfg', 'groups', ('blk', 'ulysses')), parts along dimension 1, may hold values from -6 to 6
- text_lengths: int32 [2, 2], P('cfg', 'groups'), parts along dimension 1, may hold values from 96 to 384
- timestep: int32 [2], P('groups'), parts along dimension 0, may hold values from 0 to 999
- pooled: float32 [2, 2, 2432], P(None, 'groups'), parts along dimension 1, may hold values from -6 to 6
- time_weight: bfloat16 [256, 2432], replicated, may hold values from -0.375 to 0.375
- time_second: bfloat16 [2432, 2432], P(None, ('blk', 'ulysses', 'cfg')), may hold values from -0.125 to 0.125
- mod_weight: bfloat16 [2432, 24320], P(None, ('blk', 'ulysses', 'cfg')), may hold values from -0.125 to 0.125
- proj_weight: bfloat16 [5, 2432, 2048], P(None, None, ('ulysses', 'cfg')), may hold values from -0.125 to 0.125
- out_weight: bfloat16 [2048, 2432], P(('ulysses', 'cfg')), may hold values from -0.125 to 0.125
- expand_weight: bfloat16 [2432, 7168], P('blk', ('ulysses', 'cfg')), may hold values from -0.125 to 0.125
- reduce_weight: bfloat16 [7168, 2432], P(('ulysses', 'cfg'), 'blk'), may hold values from -0.0625 to 0.0625
- qk_gain: float32 [3, 64], replicated, may hold values from 0.5 to 10
- final_weight: bfloat16 [2432, 64], replicated, may hold values from -0.125 to 0.125
Outputs:
- guided: float32 [2, 16, 128, 128], P('groups', None, ('blk', 'ulysses', 'cfg')), parts along dimension 0
There are 2 independent parts, one for each index of `groups`. A program takes and returns all parts, laid end to end along the dimension named above; an argument that names none is the same for every part. Nothing has to cross between parts.
All inputs are finite; a program needn't handle non-finite values.
Results may differ from a plain program's by a relative error of at most 0.011.
The roundings to bfloat16 on the way count: a program that leaves them out, or rounds other values in their place, can miss the bound.
Values may be sent and summed in bfloat16 or wider, within the bound.
A program may use at most 192 MiB of HBM per device.

v0:
```python
import math

import jax
import jax.numpy as jnp
from jax import lax
from jax.sharding import PartitionSpec as P

GUIDANCE = 3.5
LN_EPS = 1e-06
RMS_EPS = 1e-06
NEG_FILL = -1e30
block_keys = 512


def in_order(tiles, dim):
    shape = list(tiles.shape[1:])
    shape[dim] *= tiles.shape[0]
    return jnp.moveaxis(tiles, 0, dim).reshape(shape)


def gather_in_order(array, axes, sequence):
    tiles = array[None]
    for k in sequence:
        tiles = lax.all_gather(tiles, axes[k], axis=0, tiled=True)
    block = [lax.axis_size(axes[k]) for k in reversed(sequence)]
    tiles = tiles.reshape(*block, *array.shape)
    turned = sorted(range(len(sequence)), key=lambda place: sequence[len(sequence) - 1 - place])
    return tiles.transpose(*turned, *range(len(sequence), tiles.ndim)).reshape(-1, *array.shape)


def whole_of(array, axes, sequence, dim):
    return in_order(gather_in_order(array, axes, sequence), dim)


def gather_together(arrays, axis, dims):
    flat = jnp.concatenate([a.reshape(-1) for a in arrays])
    lines, at, outs = (lax.all_gather(flat, axis), 0, [])
    for a, dim in zip(arrays, dims):
        tiles = lines[:, at : at + a.size].reshape(-1, *a.shape)
        outs.append(in_order(tiles, dim))
        at += a.size
    return tuple(outs)


def from_everyone(array, axis):
    copies = jnp.broadcast_to(array, (lax.axis_size(axis), *array.shape))
    return lax.all_to_all(copies, axis, split_axis=0, concat_axis=0, tiled=True)


def gather_directly(array, axis, dim):
    return in_order(from_everyone(array, axis), dim)


def cut_along(array, dim, peers):
    before, after = (array.shape[:dim], array.shape[dim + 1 :])
    return jnp.moveaxis(array.reshape(*before, peers, -1, *after), dim, 0)


def sent_and_summed(array, axis, dim):
    tiles = cut_along(array, dim, lax.axis_size(axis))
    arrived = lax.all_to_all(tiles, axis, split_axis=0, concat_axis=0, tiled=True)
    return arrived.astype(jnp.float32).sum(axis=0)


def from_partner(value, axis, stride):
    mask = 2**stride
    pairs = [(source, source ^ mask) for source in range(lax.axis_size(axis))]
    return lax.ppermute(value, axis, pairs)


def sinusoid(timestep, feature_count):
    half_width = feature_count // 2
    frequency = jnp.exp(-math.log(10000.0) * jnp.arange(half_width, dtype=jnp.float32) / half_width)
    angles = timestep.astype(jnp.float32)[:, None] * frequency[None, :]
    return jnp.concatenate([jnp.cos(angles), jnp.sin(angles)], axis=1)


def layer_norm(values):
    average = jnp.mean(values, axis=-1, keepdims=True)
    centred = values - average
    variance = jnp.mean(centred * centred, axis=-1, keepdims=True)
    return centred * lax.rsqrt(variance + LN_EPS)


def modulate(values, shift, scale):
    return (layer_norm(values.astype(jnp.float32)) * (1.0 + scale) + shift).astype(jnp.bfloat16)


def rms_heads(values, gain):
    head_size = gain.shape[0]
    shaped = values.reshape(values.shape[:-1] + (values.shape[-1] // head_size, head_size))
    inverse = lax.rsqrt(jnp.mean(shaped * shaped, axis=-1, keepdims=True) + RMS_EPS)
    return (shaped * inverse * gain).reshape(values.shape).astype(jnp.bfloat16)


def finish(img_proj, txt_proj, gain_rows):
    img_set = jnp.stack(
        [
            rms_heads(img_proj[0], gain_rows[0]),
            rms_heads(img_proj[1], gain_rows[1]),
            img_proj[2].astype(jnp.bfloat16),
        ]
    )
    txt_set = jnp.stack([rms_heads(txt_proj[0], gain_rows[2]), txt_proj[1].astype(jnp.bfloat16)])
    return (img_set, txt_set)


def attend(state_now, query_heads, key_rows, value_rows, usable, scale):
    running_max, running_total, running_sum = state_now
    prompts, query_count, head_count, head_size = query_heads.shape
    key_count = key_rows.shape[1]
    key_heads = key_rows.reshape(prompts, key_count, head_count, head_size)
    value_heads = value_rows.reshape(prompts, key_count, head_count, head_size)
    scores = (
        jnp.einsum("pqhd,pkhd->phqk", query_heads, key_heads, preferred_element_type=jnp.float32)
        * scale
    )
    allowed = usable[:, None, None, :]
    block_max = jnp.max(jnp.where(allowed, scores, NEG_FILL), axis=3)
    new_max = jnp.maximum(running_max, block_max)
    weights = jnp.where(allowed, jnp.exp(scores - new_max[..., None]), 0.0)
    factor = jnp.exp(running_max - new_max)
    running_total = running_total * factor + jnp.sum(weights, axis=3)
    update = jnp.einsum(
        "phqk,pkhd->pqhd",
        weights.astype(jnp.bfloat16),
        value_heads,
        preferred_element_type=jnp.float32,
    )
    running_sum = running_sum * factor.transpose(0, 2, 1)[..., None] + update
    return (new_max, running_total, running_sum)


def attend_rows(state_now, query_heads, key_value, usable, scale):
    key_count = key_value.shape[2]
    for first_key in range(0, key_count, block_keys):
        last_key = min(first_key + block_keys, key_count)
        state_now = attend(
            state_now,
            query_heads,
            key_value[0, :, first_key:last_key],
            key_value[1, :, first_key:last_key],
            usable[:, first_key:last_key],
            scale,
        )
    return state_now


def make_fold(query_heads, lengths, img_span, txt_span, scale):
    span = img_span + txt_span

    def fold(state_now, kv_piece, first_row):
        key_count = kv_piece.shape[2]
        positions = jnp.arange(key_count, dtype=jnp.int32)
        shard_index = positions // span
        offset = positions - shard_index * span
        text_slot = shard_index * txt_span + offset - img_span
        usable = (offset < img_span)[None, :] | (text_slot[None, :] < lengths[:, None])
        return attend_rows(state_now, query_heads, kv_piece, usable, scale)

    return fold


def body(
    img_tokens,
    text_tokens,
    text_lengths,
    timestep,
    pooled,
    time_weight,
    time_second,
    mod_weight,
    proj_weight,
    out_weight,
    expand_weight,
    reduce_weight,
    qk_gain,
    final_weight,
):
    model_width = img_tokens.shape[3]
    prompts = img_tokens.shape[1]
    head_size = qk_gain.shape[1]
    branch = lax.axis_index("cfg")
    sinusoid_rows = sinusoid(timestep, time_weight.shape[0]).astype(jnp.bfloat16)
    time_hidden = jax.nn.silu(
        jnp.dot(sinusoid_rows, time_weight, preferred_element_type=jnp.float32)
    ).astype(jnp.bfloat16)
    time_part = jnp.dot(time_hidden, time_second, preferred_element_type=jnp.float32)
    time_embed = whole_of(time_part, ("blk", "ulysses", "cfg"), (1, 0, 2), 1)
    acted = jax.nn.silu(time_embed[None] + pooled).astype(jnp.bfloat16)
    mod_part = jnp.einsum("bpd,dc->bpc", acted, mod_weight, preferred_element_type=jnp.float32)
    mod_all = whole_of(mod_part, ("blk", "ulysses", "cfg"), (0, 1, 2), 2)
    own_mod = lax.dynamic_index_in_dim(mod_all, branch, 0, keepdims=False).reshape(
        prompts, 10, model_width
    )
    image_rows = img_tokens[0]
    text_rows = text_tokens[0]
    lengths = text_lengths[0]
    h_img = modulate(image_rows, own_mod[:, 0:1], own_mod[:, 1:2])
    h_txt = modulate(text_rows, own_mod[:, 4:5], own_mod[:, 3:4])
    rows_img, rows_txt = gather_together((h_img, h_txt), "ulysses", (1, 1))
    img_span = rows_img.shape[1]
    txt_span = rows_txt.shape[1]
    img_count = 3 * prompts * img_span
    weight_piece = lax.all_gather(proj_weight, "cfg", axis=2, tiled=True)
    columns = weight_piece.shape[2]
    img_part = jnp.einsum(
        "prd,jdc->jprc", rows_img, weight_piece[0:3], preferred_element_type=jnp.float32
    )
    txt_part = jnp.einsum(
        "prd,jdc->jprc", rows_txt, weight_piece[3:5], preferred_element_type=jnp.float32
    )
    stacked_rows = jnp.concatenate(
        [img_part.reshape(-1, columns), txt_part.reshape(-1, columns)], axis=0
    )
    img_proj = stacked_rows[:img_count].reshape(3, prompts, img_span, -1)
    txt_proj = stacked_rows[img_count:].reshape(2, prompts, txt_span, -1)
    img_set, txt_set = finish(img_proj, txt_proj, qk_gain)
    inner_local = img_set.shape[3]
    head_count = inner_local // head_size
    query_heads = img_set[0].reshape(prompts, img_span, head_count, head_size)
    scale = 1.0 / math.sqrt(head_size)
    start_state = (
        jnp.full((prompts, head_count, img_span), NEG_FILL, jnp.float32),
        jnp.zeros((prompts, head_count, img_span), jnp.float32),
        jnp.zeros((prompts, img_span, head_count, head_size), jnp.float32),
    )
    joined = jnp.stack(
        [
            jnp.concatenate([img_set[1], txt_set[0]], axis=1),
            jnp.concatenate([img_set[2], txt_set[1]], axis=1),
        ]
    )
    fold = make_fold(query_heads, lengths, img_span, txt_span, scale)
    final_state = fold(start_state, lax.all_gather(joined, "blk", axis=2, tiled=True), jnp.int32(0))
    running_max, running_total, running_sum = final_state
    mixed = (running_sum / running_total.transpose(0, 2, 1)[..., None]).astype(jnp.bfloat16)
    mixed_rows = mixed.reshape(prompts, img_span, inner_local).transpose(1, 0, 2)
    out_gathered = gather_directly(out_weight, "cfg", 0)
    token_count = image_rows.shape[1]
    segment = mixed_rows
    attended = sent_and_summed(
        jnp.einsum("rpc,cd->rpd", segment, out_gathered, preferred_element_type=jnp.float32).astype(
            jnp.bfloat16
        ),
        "ulysses",
        0,
    )
    attended = attended.transpose(1, 0, 2)
    residual = image_rows.astype(jnp.float32) + own_mod[:, 2:3] * attended
    feed_input = modulate(residual, own_mod[:, 7:8], own_mod[:, 8:9]).reshape(
        prompts * token_count, model_width
    )
    feed_all = gather_directly(feed_input, ("ulysses", "cfg"), 0)
    columns = feed_all
    pre_active = jnp.dot(
        columns,
        lax.all_gather(expand_weight, "blk", axis=0, tiled=True),
        preferred_element_type=jnp.float32,
    )
    feed_hidden = jax.nn.gelu(pre_active, approximate=True).astype(jnp.bfloat16)
    reduce_full = lax.all_gather(reduce_weight, "blk", axis=1, tiled=True)
    segment = feed_hidden
    feed_out = sent_and_summed(
        jnp.dot(segment, reduce_full, preferred_element_type=jnp.float32).astype(jnp.bfloat16),
        ("ulysses", "cfg"),
        0,
    )
    second_residual = residual + own_mod[:, 9:10] * feed_out.reshape(
        prompts, token_count, model_width
    )
    final_rows = modulate(second_residual, own_mod[:, 6:7], own_mod[:, 5:6])
    noise = jnp.einsum("prd,dc->prc", final_rows, final_weight, preferred_element_type=jnp.float32)
    latent_channels = final_weight.shape[1] // 4
    noise_own = noise.reshape(prompts, token_count, 2, 2, latent_channels).transpose(0, 4, 2, 1, 3)
    noise_own = noise_own.reshape(prompts, latent_channels, 2, 2 * token_count)
    kept_row = lax.dynamic_slice_in_dim(noise_own, branch, 1, 2)
    sent_row = lax.dynamic_slice_in_dim(noise_own, 1 - branch, 1, 2)
    noise_pair = from_partner(sent_row, "cfg", 0)
    noise_cond = jnp.where(branch == 0, kept_row, noise_pair)
    noise_uncond = jnp.where(branch == 0, noise_pair, kept_row)
    return noise_uncond + GUIDANCE * (noise_cond - noise_uncond)


def solution(mesh):
    in_specs = (
        P("cfg", "groups", ("blk", "ulysses"), None),
        P("cfg", "groups", ("blk", "ulysses"), None),
        P("cfg", "groups"),
        P("groups"),
        P(None, "groups", None),
        P(),
        P(None, ("blk", "ulysses", "cfg")),
        P(None, ("blk", "ulysses", "cfg")),
        P(None, None, ("ulysses", "cfg")),
        P(("ulysses", "cfg"), None),
        P("blk", ("ulysses", "cfg")),
        P(("ulysses", "cfg"), "blk"),
        P(),
        P(),
    )
    out_specs = P("groups", None, ("blk", "ulysses", "cfg"), None)
    return jax.shard_map(body, mesh=mesh, in_specs=in_specs, out_specs=out_specs, check_vma=False)
```

profile of v0, /device:TPU:33, one launch (start us, length us, event | category | flops | bytes accessed | tf_op | source)
XLA Modules:
  0.0 535.0 jit_solution(12003360434066421836)
XLA Ops:
  9.5 1.1 convert_reduce_fusion.2
  10.6 1.4 reshape.2002
  14.1 1.3 dynamic-slice
  16.3 9.7 %all-reduce = f32[76]{0:T(128)S(1)} all-reduce(f32[76]{0:T(128)S(1)} %dynamic-update-slice), channel_id=2, replica_groups=mesh['groups'=2,'blk'=16,'ulysses'=4,'cfg'=2] {'ulysses'}, use_global_device_ids=true, to_apply=%add | all-reduce | flops 76 | bytes 608
  26.0 41.2 %all_gather.37 = f32[64,1,19]{2,1,0:T(1,128)S(1)} all-gather(f32[4,1,19]{2,1,0:T(1,128)S(1)} %bitcast.553), channel_id=1, replica_groups=mesh['groups'=2,'blk'=16,'ulysses'=4,'cfg'=2] {'blk'}, dimensions={0}, use_global_device_ids=true | all-gather | bytes 5168 | tf_op jit(solution)/shard_map/all_gather | solution.py:24
  67.3 11.4 %all_gather.38 = f32[128,1,19]{2,1,0:T(1,128)S(1)} all-gather(f32[64,1,19]{2,1,0:T(1,128)S(1)} %all_gather.37), channel_id=1, replica_groups=mesh['groups'=2,'blk'=16,'ulysses'=4,'cfg'=2] {'cfg'}, dimensions={0}, use_global_device_ids=true | all-gather | bytes 14592 | tf_op jit(solution)/shard_map/all_gather | solution.py:24
  79.7 1.5 convolution_bitcast_fusion.1
  81.3 19.3 %all-gather.3 = f32[16,2,190]{2,1,0:T(2,128)S(1)} all-gather(f32[1,2,190]{2,1,0:T(2,128)S(1)} %convolution_bitcast_fusion.1), channel_id=3, replica_groups=mesh['groups'=2,'blk'=16,'ulysses'=4,'cfg'=2] {'blk'}, dimensions={0}, use_global_device_ids=true | all-gather | bytes 25840 | tf_op jit(solution)/shard_map/all_gather | solution.py:24
  100.6 9.1 %all_gather.40 = f32[64,2,1,190]{3,1,2,0:T(2,128)S(1)} all-gather(f32[16,2,1,190]{3,1,2,0:T(2,128)S(1)} %bitcast.552), channel_id=1, replica_groups=mesh['groups'=2,'blk'=16,'ulysses'=4,'cfg'=2] {'ulysses'}, dimensions={0}, use_global_device_ids=true | all-gather | bytes 121600 | tf_op jit(solution)/shard_map/all_gather | solution.py:24
  109.7 11.8 %all_gather.41 = f32[128,2,1,190]{3,1,2,0:T(2,128)S(1)} all-gather(f32[64,2,1,190]{3,1,2,0:T(2,128)S(1)} %all_gather.40), channel_id=1, replica_groups=mesh['groups'=2,'blk'=16,'ulysses'=4,'cfg'=2] {'cfg'}, dimensions={0}, use_global_device_ids=true | all-gather | bytes 291840 | tf_op jit(solution)/shard_map/all_gather | solution.py:24
  124.8 4.6 reshape.2013
  131.5 31.9 %all-gather.19.cloned.1.call-done = bf16[4,1,170240]{2,1,0:T(2,128)(2,1)} async-done(((bf16[1,1,170240]{2,1,0:T(2,128)(2,1)}), bf16[4,1,170240]{2,1,0:T(2,128)(2,1)}) %all-gather.19.cloned.1.call-update) | async-done | bytes 1361936 | tf_op jit(solution)/shard_map/all_gather | solution.py:37
  163.4 3.1 copy.201
  167.2 2.0 reshape.2023
  169.2 30.9 %all-gather.11.cloned.1.call-done = bf16[5,2432,512]{2,1,0:T(8,128)(2,1)} async-done(((bf16[5,2432,256]{2,1,0:T(8,128)(2,1)}), bf16[5,2432,512]{2,1,0:T(8,128)(2,1)}) %all-gather.11.cloned.1.call-update) | async-done | bytes 12451856 | tf_op jit(solution)/shard_map/all_gather | solution.py:205
  200.2 3.2 fusion.135
  204.0 5.3 fusion
  212.9 3.0 broadcast_in_dim.215
  215.9 5.4 %all-to-all-start = ((bf16[2,256,2432]{2,1,0:T(8,128)(2,1)}), bf16[2,256,2432]{2,1,0:T(8,128)(2,1)}, u32[]{:S(2)}, u32[]{:S(2)}) async-start(bf16[2,256,2432]{2,1,0:T(8,128)(2,1)} %broadcast_in_dim.215), calls=%async_computation | async-start | bytes 4980736 | tf_op jit(solution)/shard_map/all_to_all | solution.py:47
  223.6 100.7 %all-gather.13.cloned.1.call-done = bf16[2,1,4480,512]{3,2,1,0:T(8,128)(2,1)} async-done(((bf16[2,1,280,512]{3,2,1,0:T(8,128)(2,1)}), bf16[2,1,4480,512]{3,2,1,0:T(8,128)(2,1)}) %all-gather.13.cloned.1.call-update) | async-done | bytes 9175056 | tf_op jit(solution)/shard_map/all_gather | solution.py:235
  324.3 1.2 fusion.238
  325.7 6.0 %fusion.237 = (bf16[1,1,512,512]{3,2,1,0:T(8,128)(2,1)S(1)}, bf16[1,1,512,512]{3,2,1,0:T(8,128)(2,1)}, bf16[1,1,512,512]{3,2,1,0:T(8,128)(2,1)S(1)}, bf16[1,1,51...) fusion(bf16[2,1,4480,512]{3,2,1,0:T(8,128)(2,1)} %all-gather.13, ...), kind=kLoop, calls=%fused_computation.298 | loop fusion | bytes 16777216 | tf_op jit(solution)/shard_map/slice | solution.py:142
  331.7 2.1 copy.181
  333.7 2.0 copy.179
  335.8 2.0 copy.177
  337.8 2.0 copy.175
  339.8 2.0 copy.173
  341.9 2.0 copy.171
  343.9 2.1 copy.169
  346.0 2.1 copy.167
  348.1 2.3 select_reduce_fusion.8
  350.4 3.8 select_reduce_fusion
  354.2 2.8 select_reduce_fusion.1
  357.1 2.8 select_reduce_fusion.2
  359.9 2.7 select_reduce_fusion.3
  362.6 2.8 select_reduce_fusion.4
  365.4 2.8 select_reduce_fusion.5
  368.2 2.8 select_reduce_fusion.6
  371.0 2.7 select_reduce_fusion.7
  374.7 2.0 copy.168
  376.7 2.1 copy.170
  378.8 2.1 copy.172
  380.9 2.1 copy.174
  384.7 3.0 fusion.20
  387.7 3.6 fusion.18
  391.3 1.1 fusion.16
  392.4 1.1 fusion.14
  393.5 1.1 fusion.12
  395.0 1.1 fusion.10
  396.1 1.1 fusion.8
  397.4 1.1 fusion.6
  405.6 1.3 fusion.108
  409.0 1.1 copy-done.3
  410.1 1.1 fusion.141
  411.2 2.6 convolution_convert_fusion.1
  413.8 19.7 %all_to_all.20 = bf16[4,64,1,2432]{3,1,2,0:T(8,128)(2,1)S(1)} all-to-all(bf16[4,64,1,2432]{3,1,2,0:T(8,128)(2,1)S(1)} %bitcast.515), channel_id=1, replica_groups=mesh['groups'=2,'blk'=16,'ulysses'=4,'cfg'=2] {'ulysses'}, dimensions={0} | all-to-all | bytes 2490368 | tf_op jit(solution)/shard_map/all_to_all | solution.py:61
  434.4 1.7 broadcast_in_dim.216
  436.1 6.5 %all-to-all-start.2 = ((bf16[8,64,2432]{2,1,0:T(8,128)(2,1)}), bf16[8,64,2432]{2,1,0:T(8,128)(2,1)}, u32[]{:S(2)}, u32[]{:S(2)}) async-start(bf16[8,64,2432]{2,1,0:T(8,128)(2,1)} %broadcast_in_dim.216), calls=%async_computation.2 | async-start | bytes 4980736 | tf_op jit(solution)/shard_map/all_to_all | solution.py:47
  442.6 23.9 %all-gather.15.cloned.1.call-done = bf16[2432,896]{1,0:T(8,128)(2,1)} async-done(((bf16[152,896]{1,0:T(8,128)(2,1)}), bf16[2432,896]{1,0:T(8,128)(2,1)}) %all-gather.15.cloned.1.call-update) | async-done | bytes 4358160 | tf_op jit(solution)/shard_map/all_gather | solution.py:258
  466.5 6.7 %all-to-all-done.2 = bf16[8,64,2432]{2,1,0:T(8,128)(2,1)} async-done(((bf16[8,64,2432]{2,1,0:T(8,128)(2,1)}), bf16[8,64,2432]{2,1,0:T(8,128)(2,1)}, u32[]{:S(2)}, u32[]{:S(2)}) %all-to-all-start.2) | async-done | bytes 2490400 | tf_op jit(solution)/shard_map/all_to_all | solution.py:47
  473.2 11.5 %convolution_convert_fusion = bf16[512,2432]{1,0:T(8,128)(2,1)} fusion(bf16[896,2432]{0,1:T(8,128)(2,1)} %all-gather.17.cloned.1.call-done, bf16[512,2432]{1,0:T(8,128)(2,1)} %bitcast.123, bf16[2432,896]{1,0:T(8,128)(2,1)} %all-gather.15.cloned.1.call-done), kind=kOutput, calls=%fused_computation.5 | convolution fusion | flops 4468113408 | bytes 13697024 | tf_op jit(solution)/shard_map/dot_general | solution.py:265
  484.7 6.9 %all-to-all-start.3 = ((bf16[8,64,2432]{2,1,0:T(8,128)(2,1)}), bf16[8,64,2432]{2,1,0:T(8,128)(2,1)}, u32[]{:S(2)}, u32[]{:S(2)}) async-start(bf16[8,64,2432]{2,1,0:T(8,128)(2,1)} %bitcast.516), calls=%async_computation.3 | async-start | bytes 4980736 | tf_op jit(solution)/shard_map/all_to_all | solution.py:61
  491.7 30.6 %all-to-all-done.3 = bf16[8,64,2432]{2,1,0:T(8,128)(2,1)} async-done(((bf16[8,64,2432]{2,1,0:T(8,128)(2,1)}), bf16[8,64,2432]{2,1,0:T(8,128)(2,1)}, u32[]{:S(2)}, u32[]{:S(2)}) %all-to-all-start.3) | async-done | bytes 2490400 | tf_op jit(solution)/shard_map/all_to_all | solution.py:61
  522.3 2.1 convert_reduce_fusion
  (234 shorter events, 34.3 us)
Async XLA Ops:
  6.5 6.2 %copy-start = (bf16[256,2432]{1,0:T(8,128)(2,1)S(1)}, bf16[256,2432]{1,0:T(8,128)(2,1)}, u32[]{:S(2)}) copy-start(bf16[256,2432]{1,0:T(8,128)(2,1)} %param.19) | copy-start | bytes 3735556
  6.6 156.9 %all-gather.19.cloned.1.call-start = ((), (), s32[]{:S(2)}) async-start(), calls=%async_computation.8 | async-start | bytes 3404800 | tf_op jit(solution)/shard_map/all_gather | solution.py:37
  78.9 44.5 %copy-start.2 = (bf16[1,1,64,2432]{3,2,1,0:T(8,128)(2,1)S(1)}, bf16[1,1,64,2432]{3,2,1,0:T(8,128)(2,1)}, u32[]{:S(2)}) copy-start(bf16[1,1,64,2432]{3,2,1,0:T(8,128)(2,1)} %param.14) | copy-start | bytes 933892
  124.8 6.1 %copy-start.53 = (f32[3,64]{1,0:T(4,128)S(1)}, f32[3,64]{1,0:T(4,128)}, u32[]{:S(2)}) copy-start(f32[3,64]{1,0:T(4,128)} %param.26) | copy-start | bytes 2308
  129.5 70.6 %all-gather.11.cloned.1.call-start = ((), (), s32[]{:S(2)}) async-start(), calls=%async_computation.4 | async-start | bytes 18677760 | tf_op jit(solution)/shard_map/all_gather | solution.py:205
  130.3 194.0 %all-gather.13.cloned.1.call-start = ((), (), s32[]{:S(2)}) async-start(), calls=%async_computation.5 | async-start | bytes 9748480 | tf_op jit(solution)/shard_map/all_gather | solution.py:235
  169.2 34.8 %copy-start.19 = (bf16[256,2432,1]{1,0,2:T(8,128)(2,1)S(1)}, bf16[256,2432,1]{1,0,2:T(8,128)(2,1)}, u32[]{:S(2)}) copy-start(bf16[256,2432,1]{1,0,2:T(8,128)(2,1)} %reshape.2023) | copy-start | bytes 3735556
  212.2 230.4 %all-gather.17.cloned.1.call-start = ((), (), s32[]{:S(2)}) async-start(), calls=%async_computation.7 | async-start | bytes 4630528 | tf_op jit(solution)/shard_map/all_gather | solution.py:262
  215.9 7.6 %copy-start.52 = (f32[64]{0:T(128)S(1)}, f32[64]{0:T(128)}, u32[]{:S(2)}) copy-start(f32[64]{0:T(128)} %get-tuple-element.66) | copy-start | bytes 772
  215.9 195.3 %all-to-all-start = ((bf16[2,256,2432]{2,1,0:T(8,128)(2,1)}), bf16[2,256,2432]{2,1,0:T(8,128)(2,1)}, u32[]{:S(2)}, u32[]{:S(2)}) async-start(bf16[2,256,2432]{2,1,0:T(8,128)(2,1)} %broadcast_in_dim.215), calls=%async_computation | async-start | bytes 4980736 | tf_op jit(solution)/shard_map/all_to_all | solution.py:47
  221.3 245.2 %all-gather.15.cloned.1.call-start = ((), (), s32[]{:S(2)}) async-start(), calls=%async_computation.6 | async-start | bytes 4630528 | tf_op jit(solution)/shard_map/all_gather | solution.py:258
  222.7 125.4 %copy-start.49 = (pred[384]{0:T(512)(128)(4,1)}, pred[384]{0:T(512)(128)(4,1)S(1)}, u32[]{:S(2)}) copy-start(pred[384]{0:T(512)(128)(4,1)S(1)} %slice_reduce_fusion.14) | copy-start | bytes 1156
  222.7 127.6 %copy-start.31 = (pred[512]{0:T(512)(128)(4,1)}, pred[512]{0:T(512)(128)(4,1)S(1)}, u32[]{:S(2)}) copy-start(pred[512]{0:T(512)(128)(4,1)S(1)} %get-tuple-element.15) | copy-start | bytes 1540
  222.8 131.4 %copy-start.34 = (pred[512]{0:T(512)(128)(4,1)}, pred[512]{0:T(512)(128)(4,1)S(1)}, u32[]{:S(2)}) copy-start(pred[512]{0:T(512)(128)(4,1)S(1)} %get-tuple-element.16) | copy-start | bytes 1540
  222.8 134.3 %copy-start.37 = (pred[512]{0:T(512)(128)(4,1)}, pred[512]{0:T(512)(128)(4,1)S(1)}, u32[]{:S(2)}) copy-start(pred[512]{0:T(512)(128)(4,1)S(1)} %get-tuple-element.17) | copy-start | bytes 1540
  222.8 137.1 %copy-start.39 = (pred[512]{0:T(512)(128)(4,1)}, pred[512]{0:T(512)(128)(4,1)S(1)}, u32[]{:S(2)}) copy-start(pred[512]{0:T(512)(128)(4,1)S(1)} %get-tuple-element.18) | copy-start | bytes 1540
  222.8 139.8 %copy-start.41 = (pred[512]{0:T(512)(128)(4,1)}, pred[512]{0:T(512)(128)(4,1)S(1)}, u32[]{:S(2)}) copy-start(pred[512]{0:T(512)(128)(4,1)S(1)} %get-tuple-element.19) | copy-start | bytes 1540
  222.8 142.6 %copy-start.43 = (pred[512]{0:T(512)(128)(4,1)}, pred[512]{0:T(512)(128)(4,1)S(1)}, u32[]{:S(2)}) copy-start(pred[512]{0:T(512)(128)(4,1)S(1)} %get-tuple-element.20) | copy-start | bytes 1540
  222.8 145.4 %copy-start.45 = (pred[512]{0:T(512)(128)(4,1)}, pred[512]{0:T(512)(128)(4,1)S(1)}, u32[]{:S(2)}) copy-start(pred[512]{0:T(512)(128)(4,1)S(1)} %get-tuple-element.21) | copy-start | bytes 1540
  222.8 148.2 %copy-start.47 = (pred[512]{0:T(512)(128)(4,1)}, pred[512]{0:T(512)(128)(4,1)S(1)}, u32[]{:S(2)}) copy-start(pred[512]{0:T(512)(128)(4,1)S(1)} %get-tuple-element.22) | copy-start | bytes 1540
  348.1 6.2 %copy-start.18 = (bf16[1,1,512,512]{2,3,1,0:T(8,128)(2,1)S(1)}, bf16[1,1,512,512]{2,3,1,0:T(8,128)(2,1)}, u32[]{:S(2)}) copy-start(bf16[1,1,512,512]{2,3,1,0:T(8,128)(2,1)} %copy.179) | copy-start | bytes 1572868
  350.4 6.7 %copy-start.17 = (bf16[1,1,512,512]{2,3,1,0:T(8,128)(2,1)S(1)}, bf16[1,1,512,512]{2,3,1,0:T(8,128)(2,1)}, u32[]{:S(2)}) copy-start(bf16[1,1,512,512]{2,3,1,0:T(8,128)(2,1)} %copy.177) | copy-start | bytes 1572868
  354.2 5.7 %copy-start.16 = (bf16[1,1,512,512]{2,3,1,0:T(8,128)(2,1)S(1)}, bf16[1,1,512,512]{2,3,1,0:T(8,128)(2,1)}, u32[]{:S(2)}) copy-start(bf16[1,1,512,512]{2,3,1,0:T(8,128)(2,1)} %copy.175) | copy-start | bytes 1572868
  357.1 5.6 %copy-start.15 = (bf16[1,1,512,512]{2,3,1,0:T(8,128)(2,1)S(1)}, bf16[1,1,512,512]{2,3,1,0:T(8,128)(2,1)}, u32[]{:S(2)}) copy-start(bf16[1,1,512,512]{2,3,1,0:T(8,128)(2,1)} %copy.173) | copy-start | bytes 1572868
  359.9 5.5 %copy-start.14 = (bf16[1,1,512,512]{2,3,1,0:T(8,128)(2,1)S(1)}, bf16[1,1,512,512]{2,3,1,0:T(8,128)(2,1)}, u32[]{:S(2)}) copy-start(bf16[1,1,512,512]{2,3,1,0:T(8,128)(2,1)} %copy.171) | copy-start | bytes 1572868
  362.6 5.5 %copy-start.13 = (bf16[1,1,512,512]{2,3,1,0:T(8,128)(2,1)S(1)}, bf16[1,1,512,512]{2,3,1,0:T(8,128)(2,1)}, u32[]{:S(2)}) copy-start(bf16[1,1,512,512]{2,3,1,0:T(8,128)(2,1)} %copy.169) | copy-start | bytes 1572868
  365.4 5.6 %copy-start.12 = (bf16[1,1,512,512]{2,3,1,0:T(8,128)(2,1)S(1)}, bf16[1,1,512,512]{2,3,1,0:T(8,128)(2,1)}, u32[]{:S(2)}) copy-start(bf16[1,1,512,512]{2,3,1,0:T(8,128)(2,1)} %copy.167) | copy-start | bytes 1572868
  374.7 10.0 %copy-start.50 = (pred[384]{0:T(512)(128)(4,1)S(1)}, pred[384]{0:T(512)(128)(4,1)}, u32[]{:S(2)}) copy-start(pred[384]{0:T(512)(128)(4,1)} %copy-done.49) | copy-start | bytes 1156
  380.9 6.8 %copy-start.32 = (pred[512]{0:T(512)(128)(4,1)S(1)}, pred[512]{0:T(512)(128)(4,1)}, u32[]{:S(2)}) copy-start(pred[512]{0:T(512)(128)(4,1)} %copy-done.31) | copy-start | bytes 1540
  384.4 6.8 %copy-start.35 = (pred[512]{0:T(512)(128)(4,1)S(1)}, pred[512]{0:T(512)(128)(4,1)}, u32[]{:S(2)}) copy-start(pred[512]{0:T(512)(128)(4,1)} %copy-done.34) | copy-start | bytes 1540
  384.6 6.6 %copy-start.4 = (f32[8,256,512]{2,1,0:T(8,128)S(1)}, f32[8,256,512]{2,1,0:T(8,128)}, u32[]{:S(2)}) copy-start(f32[8,256,512]{2,1,0:T(8,128)} %get-tuple-element.74) | copy-start | bytes 12582916
  387.6 4.7 copy-start.5
  387.7 4.7 copy-start.38
  391.3 2.2 copy-start.6
  391.3 2.2 copy-start.40
  392.4 2.6 copy-start.7
  392.4 2.6 copy-start.42
  393.5 2.6 copy-start.8
  393.5 2.6 copy-start.44
  395.0 2.4 copy-start.9
  395.0 2.4 copy-start.46
  396.1 2.5 copy-start.10
  396.1 2.5 copy-start.48
  397.4 2.3 copy-start.24
  399.7 1.9 copy-start.11
  399.7 1.9 copy-start.25
  399.7 1.9 copy-start.51
  399.7 2.7 copy-start.23
  402.4 1.1 copy-start.22
  403.5 1.1 copy-start.21
  404.5 1.1 copy-start.20
  406.9 1.1 copy-start.36
  407.9 2.2 copy-start.3
  407.9 2.2 copy-start.33
  411.2 22.9 %copy-start.29 = (f32[2432]{0:T(1024)S(1)}, f32[2432]{0:T(1024)}, u32[]{:S(2)}) copy-start(f32[2432]{0:T(1024)} %get-tuple-element.8) | copy-start | bytes 29188
  411.2 22.9 %copy-start.30 = (f32[2432]{0:T(1024)S(1)}, f32[2432]{0:T(1024)}, u32[]{:S(2)}) copy-start(f32[2432]{0:T(1024)} %get-tuple-element.9) | copy-start | bytes 29188
  436.1 37.1 %all-to-all-start.2 = ((bf16[8,64,2432]{2,1,0:T(8,128)(2,1)}), bf16[8,64,2432]{2,1,0:T(8,128)(2,1)}, u32[]{:S(2)}, u32[]{:S(2)}) async-start(bf16[8,64,2432]{2,1,0:T(8,128)(2,1)} %broadcast_in_dim.216), calls=%async_computation.2 | async-start | bytes 4980736 | tf_op jit(solution)/shard_map/all_to_all | solution.py:47
  484.7 37.5 %all-to-all-start.3 = ((bf16[8,64,2432]{2,1,0:T(8,128)(2,1)}), bf16[8,64,2432]{2,1,0:T(8,128)(2,1)}, u32[]{:S(2)}, u32[]{:S(2)}) async-start(bf16[8,64,2432]{2,1,0:T(8,128)(2,1)} %bitcast.516), calls=%async_computation.3 | async-start | bytes 4980736 | tf_op jit(solution)/shard_map/all_to_all | solution.py:61
  491.6 33.3 %copy-start.26 = (bf16[2432,64]{0,1:T(8,128)(2,1)S(1)}, bf16[2432,64]{0,1:T(8,128)(2,1)}, u32[]{:S(2)}) copy-start(bf16[2432,64]{0,1:T(8,128)(2,1)} %param.27) | copy-start | bytes 933892
  491.6 33.3 %copy-start.27 = (f32[2432]{0:T(1024)S(1)}, f32[2432]{0:T(1024)}, u32[]{:S(2)}) copy-start(f32[2432]{0:T(1024)} %get-tuple-element.6) | copy-start | bytes 29188
  491.6 33.3 %copy-start.28 = (f32[2432]{0:T(1024)S(1)}, f32[2432]{0:T(1024)}, u32[]{:S(2)}) copy-start(f32[2432]{0:T(1024)} %get-tuple-element.7) | copy-start | bytes 29188
  491.6 36.4 %copy-start.1 = (bf16[256,2432]{1,0:T(8,128)(2,1)S(1)}, bf16[256,2432]{1,0:T(8,128)(2,1)}, u32[]{:S(2)}) copy-start(bf16[256,2432]{1,0:T(8,128)(2,1)} %param.19) | copy-start | bytes 3735556
  525.6 1.9 collective-permute-start
Sparse Core Ops, SparseCore 0:
  129.6 33.7 all-gather.18
  165.3 34.8 all-gather.10
  212.3 111.8 all-gather.12
  326.0 66.2 all-gather.16
  393.9 72.5 all-gather.14
where the time goes:
time: 543 us; the launch traced here: 535 us
  waiting for transfers between devices  228 us (42%)
  blocking collectives  122 us (22%)
  local copies, waits for them, and re-layouts  61.6 us (11%)
  matrix products  60.8 us (11%)
  other arithmetic  25.8 us (5%)
  starting transfers between devices  20.5 us (4%)
  between operations  16.6 us (3%)
    all_gather x1, waiting for transfers between devices, body(): lax.all_gather(joined, 'blk', axis=2, tiled=True)  101 us
    all_gather x5, blocking collectives, gather_in_order(): tiles = lax.all_gather(tiles, axes[k], axis=0, tiled=True)  92.8 us
    all_gather x1, waiting for transfers between devices, gather_together(): lines, at, outs = (lax.all_gather(flat, axis), 0, [])  31.9 us
    all_gather x1, waiting for transfers between devices, body(): weight_piece = lax.all_gather(proj_weight, 'cfg', axis=2, tiled=True)  30.9 us
    all_to_all x1, waiting for transfers between devices, sent_and_summed(): lax.all_to_all(tiles, axis, split_axis=0, concat_axis=0, tiled=True)  30.6 us
    dot_general x9, matrix products, attend(): jnp.einsum('pqhd,pkhd->phqk', query_heads, key_heads, preferred_element_t...  25.6 us
    all_gather x1, waiting for transfers between devices, body(): lax.all_gather(expand_weight, 'blk', axis=0, tiled=True)  23.9 us
    all_to_all x1, blocking collectives, sent_and_summed(): lax.all_to_all(tiles, axis, split_axis=0, concat_axis=0, tiled=True)  19.7 us
  transfers between devices with their start and end apart: 9, of which 7 were waited for; matrix products, arithmetic and copies ran while one was open for 19% of the time, Pallas kernels for 0%

commit v1 on v0

v1 whole, which is shorter than its diff:
```python
import functools
import math

import jax
import jax.numpy as jnp
from jax import lax
from jax.experimental import pallas as pl
from jax.experimental.pallas import tpu as pltpu
from jax.sharding import PartitionSpec as P

GUIDANCE = 3.5
LN_EPS = 1e-06
RMS_EPS = 1e-06
NEG_FILL = -1e30
MESH = pl.DeviceIdType.MESH
VMEM = pltpu.VMEM
BF16 = jnp.bfloat16
F32 = jnp.float32
VMEM_LIMIT = 60 * 1024 * 1024


def place():
    return lax.axis_index("blk"), lax.axis_index("ulysses"), lax.axis_index("cfg")


class Wires:
    def __init__(self, send_sems, recv_sems):
        self.send_sems, self.recv_sems, self.count, self.sent = (send_sems, recv_sems, 0, [])

    def send(self, src, dst, **device):
        number = self.count
        self.count += 1
        copy = pltpu.make_async_remote_copy(
            src_ref=src,
            dst_ref=dst,
            send_sem=self.send_sems.at[number],
            recv_sem=self.recv_sems.at[number],
            device_id=device,
            device_id_type=MESH,
        )
        copy.start()
        self.sent.append(copy)
        return number

    def arrive(self, number, dst, **device):
        pltpu.make_async_remote_copy(
            src_ref=dst,
            dst_ref=dst,
            send_sem=self.send_sems.at[number],
            recv_sem=self.recv_sems.at[number],
            device_id=device,
            device_id_type=MESH,
        ).wait_recv()

    def drain(self):
        for copy in self.sent:
            copy.wait_send()
        self.sent = []


def greet(devices):
    barrier = pltpu.get_barrier_semaphore()
    for device in devices:
        pl.semaphore_signal(barrier, inc=1, device_id=device, device_id_type=MESH)
    pl.semaphore_wait(barrier, len(devices))


def ring_greetings(u, c, nu):
    return [
        {"ulysses": lax.rem(u + 1, nu)},
        {"ulysses": lax.rem(u + nu - 1, nu)},
        {"cfg": 1 - c},
    ]


def sinusoid(timestep, feature_count):
    half_width = feature_count // 2
    frequency = jnp.exp(-math.log(10000.0) * jnp.arange(half_width, dtype=F32) / half_width)
    angles = timestep.astype(F32)[:, None] * frequency[None, :]
    return jnp.concatenate([jnp.cos(angles), jnp.sin(angles)], axis=1)


def normalized(values, shift, scale):
    average = jnp.mean(values, axis=-1, keepdims=True)
    centred = values - average
    variance = jnp.mean(centred * centred, axis=-1, keepdims=True)
    return centred * lax.rsqrt(variance + LN_EPS) * (1.0 + scale) + shift


def spread_kernel(nb, nu, own_branch, part_ref, out_ref, buf, send1, recv1, send2, recv2, local_sem):
    b, u, c = place()
    per = 2 * nu
    me = u * 2 + c
    greet(
        [{"ulysses": lax.rem(me + k, per) // 2, "cfg": lax.rem(me + k, per) % 2} for k in range(1, per)]
        + [{"blk": lax.rem(b + k, nb)} for k in range(1, nb)]
    )
    near, far = (Wires(send1, recv1), Wires(send2, recv2))
    own = pltpu.make_async_copy(part_ref.at[c if own_branch else 0], buf.at[b, me], local_sem)
    own.start()
    for k in range(1, per):
        peer = lax.rem(me + k, per)
        near.send(
            part_ref.at[peer % 2 if own_branch else 0],
            buf.at[b, me],
            ulysses=peer // 2,
            cfg=peer % 2,
        )
    own.wait()
    for k in range(1, per):
        peer = lax.rem(me + per - k, per)
        near.arrive(k - 1, buf.at[b, peer], ulysses=peer // 2, cfg=peer % 2)
    for k in range(1, nb):
        far.send(buf.at[b], buf.at[b], blk=lax.rem(b + k, nb))
    for k in range(1, nb):
        peer = lax.rem(b + nb - k, nb)
        far.arrive(k - 1, buf.at[peer], blk=peer)
    near.drain()
    far.drain()
    out_ref[...] = buf[...]


def spread(mesh, part, own_branch, call_id):
    nb, nu = (mesh.shape["blk"], mesh.shape["ulysses"])
    width = part.shape[2]
    return pl.pallas_call(
        functools.partial(spread_kernel, nb, nu, own_branch),
        out_shape=jax.ShapeDtypeStruct((nb, 2 * nu, 1, width), F32),
        in_specs=[pl.BlockSpec(memory_space=VMEM)],
        out_specs=pl.BlockSpec(memory_space=VMEM),
        scratch_shapes=[
            VMEM((nb, 2 * nu, 1, width), F32),
            pltpu.SemaphoreType.DMA((2 * nu,)),
            pltpu.SemaphoreType.DMA((2 * nu,)),
            pltpu.SemaphoreType.DMA((nb,)),
            pltpu.SemaphoreType.DMA((nb,)),
            pltpu.SemaphoreType.DMA,
        ],
        compiler_params=pltpu.CompilerParams(collective_id=call_id, has_side_effects=True),
        name=f"spread_{call_id}",
    )(part)


def ring_share(wires, first, second, u, c, nu):
    right, left, opposite = (lax.rem(u + 1, nu), lax.rem(u + nu - 1, nu), lax.rem(u + 2, nu))
    slot = lambda uu, cc: cc * nu + uu
    mine, other = (slot(u, c), 1 - c)
    across = {}

    def push(view, where, **device):
        return wires.send(view(where), view(where), **device)

    go_right, go_left = ({}, {})
    for view in first + second:
        go_right[view] = push(view, mine, ulysses=right)
    for view in second + first:
        go_left[view] = push(view, mine, ulysses=left)
    for view in first + second:
        across[view, "mine"] = push(view, mine, cfg=other)
    on_right, on_left = ({}, {})
    for k in range(len(first + second)):
        for views, got, came, onward, far in (
            (first + second, go_right, left, on_right, first),
            (second + first, go_left, right, on_left, second),
        ):
            if k >= len(views):
                continue
            view = views[k]
            wires.arrive(got[view], view(slot(came, c)), ulysses=came)
            if view in far:
                onward[view] = push(view, slot(came, c), ulysses=right if got is go_right else left)
            across[view, "left" if got is go_right else "right"] = push(view, slot(came, c), cfg=other)
    for view in first + second:
        forward, came = (on_right, left) if view in first else (on_left, right)
        wires.arrive(forward[view], view(slot(opposite, c)), ulysses=came)
        across[view, "opposite"] = push(view, slot(opposite, c), cfg=other)
    for (view, source), number in across.items():
        uu = {"mine": u, "left": left, "right": right, "opposite": opposite}[source]
        wires.arrive(number, view(slot(uu, other)), cfg=other)


def project_kernel(nu, img_ref, txt_ref, mod_ref, gain_ref, w_ref, out_ref, himg, htxt, w_buf, stage, send, recv, local):
    b, u, c = place()
    rows, depth = img_ref.shape
    text_rows = txt_ref.shape[0]
    load = pltpu.make_async_copy(w_ref, w_buf, local)
    load.start()
    mine = c * nu + u
    half = rows // 2
    for part in range(2):
        span = pl.ds(part * half, half)
        himg[mine, span] = normalized(
            img_ref[span].astype(F32), mod_ref[0:1], mod_ref[1:2]
        ).astype(BF16)
    htxt[...] = jnp.zeros_like(htxt)
    htxt[mine, 0:text_rows] = normalized(
        txt_ref[...].astype(F32), mod_ref[4:5], mod_ref[3:4]
    ).astype(BF16)
    greet(ring_greetings(u, c, nu))
    wires = Wires(send, recv)
    ring_share(
        wires,
        [lambda s: himg.at[s, pl.ds(0, half)], lambda s: htxt.at[s, pl.ds(0, 8)]],
        [lambda s: himg.at[s, pl.ds(half, half)]],
        u,
        c,
        nu,
    )
    load.wait()
    width = w_buf.shape[2]
    heads = width // 64
    lane = lax.broadcasted_iota(jnp.int32, (width, width), 0) // 64
    group = jnp.where(lane == lax.broadcasted_iota(jnp.int32, (width, width), 1) // 64, 1.0 / 64, 0.0)

    def unit(values, gain):
        square = values * values
        high = square.astype(BF16)
        low = (square - high.astype(F32)).astype(BF16)
        ones = group.astype(BF16)
        mean = jnp.dot(high, ones, preferred_element_type=F32) + jnp.dot(
            low, ones, preferred_element_type=F32
        )
        return values * lax.rsqrt(mean + RMS_EPS) * gain

    img_span = nu * rows
    for branch in range(2):
        x = himg[pl.ds(branch * nu, nu)].reshape(img_span, depth)
        q = unit(jnp.dot(x, w_buf[0], preferred_element_type=F32), gain_ref[0:1]) * 0.125
        q = q.astype(BF16).astype(F32)
        for h in range(heads):
            pair, odd = (h // 2, h % 2)
            block = q[:, pair * 128 : pair * 128 + 128]
            turned = pltpu.roll(block, 64, 1)
            low, high = (turned, block) if odd else (block, turned)
            lanes = lax.broadcasted_iota(jnp.int32, (img_span // 2, 128), 1)
            out_ref[branch * heads + h, pl.ds(img_span + 32, img_span // 2)] = jnp.where(
                lanes < 64, low[: img_span // 2], high[img_span // 2 :]
            ).astype(BF16)
        k = unit(jnp.dot(x, w_buf[1], preferred_element_type=F32), gain_ref[1:2])
        v = jnp.dot(x, w_buf[2], preferred_element_type=F32)
        t = htxt[pl.ds(branch * nu, nu)].reshape(nu * 16, depth)
        tk = unit(jnp.dot(t, w_buf[3], preferred_element_type=F32), gain_ref[2:3])
        tv = jnp.dot(t, w_buf[4], preferred_element_type=F32)
        for keys, values, at, live in ((k, v, 0, None), (tk, tv, img_span, 8)):
            for h in range(heads):
                pair, odd = (h // 2, h % 2)
                kb = keys[:, pair * 128 : pair * 128 + 128]
                vb = values[:, pair * 128 : pair * 128 + 128]
                kb = pltpu.roll(kb, 64, 1) if odd else kb
                vb = vb if odd else pltpu.roll(vb, 64, 1)
                lanes = lax.broadcasted_iota(jnp.int32, kb.shape, 1)
                both = jnp.where(lanes < 64, kb, vb)
                if live is not None:
                    both = jnp.concatenate([both[i * 16 : i * 16 + live] for i in range(nu)], axis=0)
                out_ref[branch * heads + h, pl.ds(at, both.shape[0])] = both.astype(BF16)
    wires.drain()


def project(mesh, img, txt, mod, gain, weights):
    nu = mesh.shape["ulysses"]
    rows, depth = img.shape
    width = weights.shape[2]
    units = 2 * (width // 64)
    vm = pl.BlockSpec(memory_space=VMEM)
    return pl.pallas_call(
        functools.partial(project_kernel, nu),
        out_shape=jax.ShapeDtypeStruct((units, nu * rows + 32 + nu * rows // 2, 128), BF16),
        in_specs=[vm, vm, vm, vm, pl.BlockSpec(memory_space=pl.ANY)],
        out_specs=vm,
        scratch_shapes=[
            VMEM((2 * nu, rows, depth), BF16),
            VMEM((2 * nu, 16, depth), BF16),
            VMEM(weights.shape, BF16),
            VMEM((8, 128), F32),
            pltpu.SemaphoreType.DMA((32,)),
            pltpu.SemaphoreType.DMA((32,)),
            pltpu.SemaphoreType.DMA,
        ],
        compiler_params=pltpu.CompilerParams(
            collective_id=2, has_side_effects=True, vmem_limit_bytes=VMEM_LIMIT
        ),
        name="project",
    )(img, txt, mod, gain, weights)


def attend_kernel(
    nb, nu, unit_ref, bias_ref, wo_ref, out_ref,
    kvb, qb, k_t, kv1, scores, stage, heads_in, wo, mixed,
    kv_send, kv_recv, q_send, q_recv, f_send, f_recv, o_send, o_recv, w_send, w_recv, local, local_w,
):
    b, u, c = place()
    other = 1 - c
    side = lax.rem(b, 2)
    units = unit_ref.shape[0]
    kv_rows = kvb.shape[1]
    img_span = kv_rows - 32
    q_rows = qb.shape[1]
    tiles = qb.shape[0]
    branch = b // (nb // 2)
    peers = [{"blk": lax.rem(b + k, nb), "cfg": cc} for k in range(1, nb) for cc in range(2)]
    load_w = pltpu.make_async_copy(wo_ref, wo.at[c], local_w)
    load_w.start()
    greet(peers + [{"cfg": other}])

    def kv_copy(i, blk, core, src):
        return pltpu.make_async_remote_copy(
            src_ref=src, dst_ref=kvb.at[b], send_sem=kv_send.at[i], recv_sem=kv_recv.at[b // 2],
            device_id={"blk": blk, "cfg": core}, device_id_type=MESH,
        )

    def q_copy(i, blk, core, src):
        return pltpu.make_async_remote_copy(
            src_ref=src, dst_ref=qb.at[b // 2], send_sem=q_send.at[i], recv_sem=q_recv.at[b // 2],
            device_id={"blk": blk, "cfg": core}, device_id_type=MESH,
        )

    def local_kv(i):
        return pltpu.make_async_copy(unit_ref.at[i, pl.ds(0, kv_rows)], kvb.at[2 * i + c], local.at[0])

    def local_q(i):
        return pltpu.make_async_copy(unit_ref.at[i, pl.ds(kv_rows, q_rows)], qb.at[i], local.at[1])

    for i in range(units):
        blk = 2 * i + c

        @pl.when(blk != b)
        def _():
            kv_copy(i, blk, side, unit_ref.at[i, pl.ds(0, kv_rows)]).start()
            q_copy(i, blk, side, unit_ref.at[i, pl.ds(kv_rows, q_rows)]).start()

        @pl.when(blk == b)
        def _():
            local_kv(i).start()
            local_q(i).start()

    load_w.wait()
    share_w = pltpu.make_async_remote_copy(
        src_ref=wo.at[c], dst_ref=wo.at[c], send_sem=w_send, recv_sem=w_recv,
        device_id={"cfg": other}, device_id_type=MESH,
    )
    share_w.start()

    def arrival(ref, sem, blk):
        return pltpu.make_async_remote_copy(
            src_ref=ref, dst_ref=ref, send_sem=kv_send.at[0], recv_sem=sem,
            device_id={"blk": blk, "cfg": side}, device_id_type=MESH,
        )

    def forward(i, blk):
        return pltpu.make_async_remote_copy(
            src_ref=kvb.at[blk], dst_ref=kvb.at[blk], send_sem=f_send.at[i], recv_sem=f_recv.at[i],
            device_id={"cfg": other}, device_id_type=MESH,
        )

    def prepare(blk):
        rows = kvb[blk]
        image = rows[:img_span]
        at = pl.multiple_of(blk * img_span, img_span)
        k_t[:, pl.ds(at, img_span)] = image.astype(F32).T.astype(BF16)
        lanes = lax.broadcasted_iota(jnp.int32, rows.shape, 1)
        ones = jnp.where(lanes < 64, jnp.ones_like(rows), rows)
        kv1[pl.ds(at, img_span)] = ones[:img_span]
        low = pl.multiple_of(nb * img_span + blk * 32, 32)
        kv1[pl.ds(low, 32)] = ones[img_span:]

    for i in range(units):
        blk = 2 * i + c

        @pl.when(blk != b)
        def _():
            arrival(kvb.at[blk], kv_recv.at[i], blk).wait_recv()

        @pl.when(blk == b)
        def _():
            local_kv(i).wait()

        forward(i, blk).start()
        prepare(blk)
    for i in range(units):
        blk = 2 * i + other
        forward(i, blk).wait_recv()
        prepare(blk)
    text = jnp.concatenate([kvb[k, img_span:kv_rows] for k in range(nb)], axis=0)
    text_at = nb * img_span
    text_keys = nb * 32
    k_t[:, text_at : text_at + text_keys] = text.astype(F32).T.astype(BF16)
    for i in range(units):
        blk = 2 * i + c

        @pl.when(blk != b)
        def _():
            arrival(qb.at[i], q_recv.at[i], blk).wait_recv()

        @pl.when(blk == b)
        def _():
            local_q(i).wait()

    key_count = text_at + text_keys
    step = 512
    lanes = lax.broadcasted_iota(jnp.int32, (q_rows, 128), 1)
    head = side * 4 + lax.rem(b // 2, 4)

    def o_copy(i, blk):
        return pltpu.make_async_remote_copy(
            src_ref=stage.at[i], dst_ref=heads_in.at[head], send_sem=o_send.at[i], recv_sem=o_recv.at[head],
            device_id={"blk": blk, "cfg": branch}, device_id_type=MESH,
        )

    def o_local(i):
        return pltpu.make_async_copy(stage.at[i], heads_in.at[head], local.at[0])

    @pl.loop(0, tiles)
    def _(i):
        packed = qb[i].astype(F32)
        low = jnp.where(lanes < 64, packed, 0.0)
        high = jnp.where(lanes < 64, pltpu.roll(packed, 64, 1), 0.0)
        q = jnp.concatenate([low, high], axis=0).astype(BF16)
        top = jnp.full((2 * q_rows, 128), NEG_FILL, F32)
        for at in range(0, key_count, step):
            block = jnp.dot(q, k_t[:, at : at + step], preferred_element_type=F32)
            if at >= text_at:
                block = block + bias_ref[branch, :, at - text_at : at - text_at + step]
            scores[:, at : at + step] = block
            for piece in range(0, step, 128):
                top = jnp.maximum(top, block[:, piece : piece + 128])
        row_max = jnp.max(top, axis=1, keepdims=True)
        total = jnp.zeros((2 * q_rows, 128), F32)
        for at in range(0, key_count, step):
            weights = jnp.exp(scores[:, at : at + step] - row_max).astype(BF16)
            total = total + jnp.dot(weights, kv1[at : at + step], preferred_element_type=F32)
        turned = pltpu.roll(total, 64, 1)
        first = turned[:q_rows] / total[:q_rows]
        second = total[q_rows:] / turned[q_rows:]
        stage[i] = jnp.where(lanes < 64, first, second).astype(BF16)
        blk = 2 * i + c
        mine = jnp.logical_and(blk == b, branch == c)

        @pl.when(mine)
        def _():
            o_local(i).start()

        @pl.when(jnp.logical_not(mine))
        def _():
            o_copy(i, blk).start()

    share_w.wait_recv()
    for h in range(8):
        source = (nb // 2) * c + 2 * (h % 4) + h // 4
        mine = jnp.logical_and(source == b, side == c)

        @pl.when(mine)
        def _():
            pltpu.make_async_copy(stage.at[0], heads_in.at[h], local.at[0]).wait()

        @pl.when(jnp.logical_not(mine))
        def _():
            pltpu.make_async_remote_copy(
                src_ref=heads_in.at[h], dst_ref=heads_in.at[h], send_sem=o_send.at[0], recv_sem=o_recv.at[h],
                device_id={"blk": source, "cfg": side}, device_id_type=MESH,
            ).wait_recv()

    for pair in range(4):
        even = heads_in[2 * pair].astype(F32)
        odd = heads_in[2 * pair + 1].astype(F32)
        span = slice(pair * 128, pair * 128 + 128)
        mixed[0:q_rows, span] = jnp.where(lanes < 64, even, pltpu.roll(odd, 64, 1)).astype(BF16)
        mixed[q_rows : 2 * q_rows, span] = jnp.where(lanes < 64, pltpu.roll(even, 64, 1), odd).astype(BF16)
    weight_rows = wo.shape[0] * wo.shape[1]
    out = jnp.dot(
        mixed[...], wo[...].reshape(weight_rows, wo.shape[2]), preferred_element_type=F32
    ).astype(BF16)
    out_ref[...] = out.reshape(out_ref.shape)
    share_w.wait_send()
    for i in range(units):
        blk = 2 * i + c

        @pl.when(blk != b)
        def _():
            kv_copy(i, blk, side, unit_ref.at[i, pl.ds(0, kv_rows)]).wait_send()
            q_copy(i, blk, side, unit_ref.at[i, pl.ds(kv_rows, q_rows)]).wait_send()

        forward(i, blk).wait_send()

        @pl.when(jnp.logical_not(jnp.logical_and(blk == b, branch == c)))
        def _():
            o_copy(i, blk).wait_send()


def attention(mesh, unit_rows, bias, out_weight, rows):
    nb, nu = (mesh.shape["blk"], mesh.shape["ulysses"])
    units = unit_rows.shape[0]
    img_span = nu * rows
    q_rows = img_span // 2
    kv_rows = img_span + 32
    keys = nb * kv_rows
    depth = out_weight.shape[1]
    dma = pltpu.SemaphoreType.DMA
    vm = pl.BlockSpec(memory_space=VMEM)
    return pl.pallas_call(
        functools.partial(attend_kernel, nb, nu),
        out_shape=jax.ShapeDtypeStruct((nu, rows, depth), BF16),
        in_specs=[vm, vm, pl.BlockSpec(memory_space=pl.ANY)],
        out_specs=vm,
        scratch_shapes=[
            VMEM((nb, kv_rows, 128), BF16),
            VMEM((units, q_rows, 128), BF16),
            VMEM((128, keys), BF16),
            VMEM((keys, 128), BF16),
            VMEM((2 * q_rows, keys), F32),
            VMEM((units, q_rows, 128), BF16),
            VMEM((8, q_rows, 128), BF16),
            VMEM((2, *out_weight.shape), BF16),
            VMEM((2 * q_rows, 512), BF16),
            dma((units,)), dma((units,)), dma((units,)), dma((units,)), dma((units,)), dma((units,)),
            dma((units,)), dma((8,)), dma, dma, dma((2,)), dma,
        ],
        compiler_params=pltpu.CompilerParams(
            collective_id=3, has_side_effects=True, vmem_limit_bytes=VMEM_LIMIT
        ),
        name="attend",
    )(unit_rows, bias, out_weight)


def ring_sum(wires, part, relay, staged, inbox, u, nu, emit):
    right, left, opposite = (lax.rem(u + 1, nu), lax.rem(u + nu - 1, nu), lax.rem(u + 2, nu))
    half = part.shape[1] // 2
    low, high = (pl.ds(0, half), pl.ds(half, half))
    far_r = wires.send(part.at[opposite, low], relay.at[0], ulysses=right)
    far_l = wires.send(part.at[opposite, high], relay.at[1], ulysses=left)
    near_r = wires.send(part.at[right, high], inbox.at[0, high], ulysses=right)
    near_l = wires.send(part.at[left, low], inbox.at[1, low], ulysses=left)
    wires.arrive(far_r, relay.at[0], ulysses=left)
    staged[0] = (part[right, low].astype(F32) + relay[0].astype(F32)).astype(BF16)
    last_r = wires.send(staged.at[0], inbox.at[0, low], ulysses=right)
    wires.arrive(far_l, relay.at[1], ulysses=right)
    staged[1] = (part[left, high].astype(F32) + relay[1].astype(F32)).astype(BF16)
    last_l = wires.send(staged.at[1], inbox.at[1, high], ulysses=left)
    wires.arrive(near_r, inbox.at[0, high], ulysses=left)
    wires.arrive(near_l, inbox.at[1, low], ulysses=right)
    wires.arrive(last_r, inbox.at[0, low], ulysses=left)
    wires.arrive(last_l, inbox.at[1, high], ulysses=right)

    @pl.loop(0, part.shape[1], step=16)
    def _(at):
        span = pl.ds(pl.multiple_of(at, 16), 16)
        total = part[u, span].astype(F32) + inbox[0, span].astype(F32) + inbox[1, span].astype(F32)
        emit(span, total)


def middle_kernel(nu, part, img_ref, mod_ref, all_ref, res_ref, relay, staged, inbox, feed, send, recv):
    b, u, c = place()
    greet(ring_greetings(u, c, nu))
    wires = Wires(send, recv)
    mine = c * nu + u
    half = part.shape[1] // 2

    def emit(span, total):
        residual = img_ref[span].astype(F32) + mod_ref[2:3] * total
        res_ref[span] = residual
        feed[mine, span] = normalized(residual, mod_ref[7:8], mod_ref[8:9]).astype(BF16)

    ring_sum(wires, part, relay, staged, inbox, u, nu, emit)
    ring_share(
        wires,
        [lambda s: feed.at[s, pl.ds(0, half)]],
        [lambda s: feed.at[s, pl.ds(half, half)]],
        u,
        c,
        nu,
    )
    all_ref[...] = feed[...]
    wires.drain()


def middle(mesh, part, img, mod):
    nu = mesh.shape["ulysses"]
    rows, depth = img.shape
    vm = pl.BlockSpec(memory_space=VMEM)
    return pl.pallas_call(
        functools.partial(middle_kernel, nu),
        out_shape=(
            jax.ShapeDtypeStruct((2 * nu, rows, depth), BF16),
            jax.ShapeDtypeStruct((rows, depth), F32),
        ),
        in_specs=[vm, vm, vm],
        out_specs=(vm, vm),
        scratch_shapes=[
            VMEM((2, rows // 2, depth), BF16),
            VMEM((2, rows // 2, depth), BF16),
            VMEM((2, rows, depth), BF16),
            VMEM((2 * nu, rows, depth), BF16),
            pltpu.SemaphoreType.DMA((32,)),
            pltpu.SemaphoreType.DMA((32,)),
        ],
        compiler_params=pltpu.CompilerParams(
            collective_id=4, has_side_effects=True, vmem_limit_bytes=VMEM_LIMIT
        ),
        name="middle",
    )(part, img, mod)


def last_kernel(
    nu, part, res_ref, mod_ref, fw_ref, out_ref, cross, summed, relay, staged, inbox, final, noise, send, recv
):
    b, u, c = place()
    greet(ring_greetings(u, c, nu))
    wires = Wires(send, recv)
    other = 1 - c
    right, left, opposite = (lax.rem(u + 1, nu), lax.rem(u + nu - 1, nu), lax.rem(u + 2, nu))
    order = (opposite, right, left, u)
    numbers = [wires.send(part.at[other, k], cross.at[k], cfg=other) for k in order]
    for number, k in zip(numbers, order):
        wires.arrive(number, cross.at[k], cfg=other)

        @pl.loop(0, part.shape[2], step=16)
        def _(at):
            span = pl.ds(pl.multiple_of(at, 16), 16)
            summed[k, span] = (part[c, k, span].astype(F32) + cross[k, span].astype(F32)).astype(BF16)

    def emit(span, total):
        second = res_ref[span] + mod_ref[9:10] * total
        final[span] = normalized(second, mod_ref[6:7], mod_ref[5:6]).astype(BF16)

    ring_sum(wires, summed, relay, staged, inbox, u, nu, emit)
    noise[c] = lax.dot_general(
        final[...], fw_ref[...], (((1,), (1,)), ((), ())), preferred_element_type=F32
    )
    swap = wires.send(noise.at[c], noise.at[c], cfg=other)
    wires.arrive(swap, noise.at[other], cfg=other)
    out_ref[...] = noise[1] + GUIDANCE * (noise[0] - noise[1])
    wires.drain()


def last(mesh, part, residual, mod, final_weight_t):
    nu = mesh.shape["ulysses"]
    rows, depth = residual.shape
    vm = pl.BlockSpec(memory_space=VMEM)
    return pl.pallas_call(
        functools.partial(last_kernel, nu),
        out_shape=jax.ShapeDtypeStruct((rows, 128), F32),
        in_specs=[vm, vm, vm, vm],
        out_specs=vm,
        scratch_shapes=[
            VMEM((nu, rows, depth), BF16),
            VMEM((nu, rows, depth), BF16),
            VMEM((2, rows // 2, depth), BF16),
            VMEM((2, rows // 2, depth), BF16),
            VMEM((2, rows, depth), BF16),
            VMEM((rows, depth), BF16),
            VMEM((2, rows, 128), F32),
            pltpu.SemaphoreType.DMA((16,)),
            pltpu.SemaphoreType.DMA((16,)),
        ],
        compiler_params=pltpu.CompilerParams(
            collective_id=5, has_side_effects=True, vmem_limit_bytes=VMEM_LIMIT
        ),
        name="last",
    )(part, residual, mod, final_weight_t)


def body(
    mesh,
    img_tokens,
    text_tokens,
    text_lengths,
    timestep,
    pooled,
    time_weight,
    time_second,
    mod_weight,
    proj_weight,
    out_weight,
    expand_weight,
    reduce_weight,
    qk_gain,
    final_weight,
):
    depth = img_tokens.shape[3]
    nb, nu = (mesh.shape["blk"], mesh.shape["ulysses"])
    image = img_tokens[0, 0]
    text = text_tokens[0, 0]
    rows, text_rows = (image.shape[0], text.shape[0])
    branch = lax.axis_index("cfg")
    expand_full = lax.all_gather(expand_weight, "blk", axis=0, tiled=True)
    reduce_full_t = lax.all_gather(reduce_weight.T, "blk", axis=0, tiled=True)

    sinusoid_rows = sinusoid(timestep, time_weight.shape[0]).astype(BF16)
    time_hidden = jax.nn.silu(
        jnp.dot(sinusoid_rows, time_weight, preferred_element_type=F32)
    ).astype(BF16)
    time_part = jnp.dot(time_hidden, time_second, preferred_element_type=F32)
    share = time_part.shape[1]
    row = jnp.concatenate([time_part, text_lengths.astype(F32)], axis=1)
    row = jnp.pad(row, ((0, 0), (0, 127 - share)))[None]
    times = spread(mesh, row, False, 0)
    time_embed = times[:, :, 0, :share].reshape(1, depth)
    lengths = times[0, 0:2, 0, share]
    acted = jax.nn.silu(time_embed + pooled[:, 0]).astype(BF16)
    mod_part = jnp.dot(acted, mod_weight, preferred_element_type=F32)
    columns = mod_part.shape[1]
    mod_rows = jnp.pad(mod_part, ((0, 0), (0, 256 - columns)))[:, None]
    mod = spread(mesh, mod_rows, True, 1)[:, :, 0, :columns].reshape(10, depth)

    position = jnp.arange(nb * 32, dtype=jnp.int32)
    within = position % 8
    slot = (position // 32) * (nu * text_rows) + (position % 32) // 8 * text_rows + within
    allowed = (within < text_rows)[None] & (slot[None].astype(F32) < lengths[:, None])
    bias = jnp.where(allowed, 0.0, NEG_FILL).astype(F32)[:, None]

    heads = proj_weight.shape[2] // qk_gain.shape[1]
    gain = jnp.tile(qk_gain, (1, heads))
    unit_rows = project(mesh, image, text, mod, gain, proj_weight)
    part = attention(mesh, unit_rows, bias, out_weight, rows)
    feed_all, residual = middle(mesh, part, image, mod)
    pre_active = jnp.dot(
        feed_all.reshape(-1, depth), expand_full, preferred_element_type=F32
    )
    feed_hidden = jax.nn.gelu(pre_active, approximate=True).astype(BF16)
    feed_part = lax.dot_general(
        feed_hidden, reduce_full_t, (((1,), (1,)), ((), ())), preferred_element_type=F32
    ).astype(BF16)
    final_t = jnp.pad(final_weight.T, ((0, 128 - final_weight.shape[1]), (0, 0)))
    guided = last(mesh, feed_part.reshape(2, nu, rows, depth), residual, mod, final_t)
    channels = final_weight.shape[1] // 4
    own = lax.dynamic_slice_in_dim(guided, branch * 2 * channels, 2 * channels, 1)
    own = own.reshape(rows, 2, channels).transpose(2, 0, 1)
    return own.reshape(1, channels, 1, 2 * rows)


def solution(mesh):
    in_specs = (
        P("cfg", "groups", ("blk", "ulysses"), None),
        P("cfg", "groups", ("blk", "ulysses"), None),
        P("cfg", "groups"),
        P("groups"),
        P(None, "groups", None),
        P(),
        P(None, ("blk", "ulysses", "cfg")),
        P(None, ("blk", "ulysses", "cfg")),
        P(None, None, ("ulysses", "cfg")),
        P(("ulysses", "cfg"), None),
        P("blk", ("ulysses", "cfg")),
        P(("ulysses", "cfg"), "blk"),
        P(),
        P(),
    )
    out_specs = P("groups", None, ("blk", "ulysses", "cfg"), None)
    return jax.shard_map(
        functools.partial(body, mesh), mesh=mesh, in_specs=in_specs, out_specs=out_specs, check_vma=False
    )
```

time: 543 us -> 258 us (0.48); the launches traced: 535 us -> 258 us
  waiting for transfers between devices: 228 us -> 2.87 us
  Pallas kernels: 0 us -> 218 us
  blocking collectives: 122 us -> 0 us
  local copies, waits for them, and re-layouts: 61.6 us -> 8.09 us
  matrix products: 60.8 us -> 12.3 us
  other arithmetic: 25.8 us -> 1.36 us
  starting transfers between devices: 20.5 us -> 0.12 us
    pallas_call x0 -> x6, Pallas kernels: none -> 218 us  [the longest x1 75.5 us: attention(): pl.pallas_call(functools.partial(attend_kernel, nb, nu), out_shape=jax.Sh...]
    all_gather x5 -> x2, waiting for transfers between devices: 187 us -> 1.43 us  [the longest x1 1.43 us: body(): reduce_full_t = lax.all_gather(reduce_weight.T, 'blk', axis=0, tiled=True)]
    all_gather x5 -> x0, blocking collectives: 92.8 us -> none  [gather_in_order(): tiles = lax.all_gather(tiles, axes[k], axis=0, tiled=True)]
    dot_general x26 -> x4, matrix products: 60.8 us -> 12.3 us  [the longest x1 11.5 us: body(): lax.dot_general(feed_hidden, reduce_full_t, (((1,), (1,)), ((), ())), pre...]
    all_to_all x3 -> x0, waiting for transfers between devices: 37.3 us -> none  [the longest x1 30.6 us: sent_and_summed(): lax.all_to_all(tiles, axis, split_axis=0, concat_axis=0, tiled=True)]
    slice x25 -> x3, local copies, waits for them, and re-layouts: 35.4 us -> 3.1 us  [the longest x1 1.25 us: body(): mod = spread(mesh, mod_rows, True, 1)[:, :, 0, :columns].reshape(10, depth)]
    reduce_sum x22 -> x0, other arithmetic: 20.9 us -> none  [the longest x9 14.1 us: attend(): running_total = running_total * factor + jnp.sum(weights, axis=3)]
    all_to_all x1 -> x0, blocking collectives: 19.7 us -> none  [sent_and_summed(): lax.all_to_all(tiles, axis, split_axis=0, concat_axis=0, tiled=True)]
  transfers between devices with their start and end apart: 9 -> 2, of which waited for: 7 -> 1; matrix products, arithmetic and copies ran while one was open for 19% -> 3% of each run, Pallas kernels for 0% -> 75%
where the time goes in v1:
time: 258 us
  Pallas kernels  218 us (84%)
  between operations  14.9 us (6%)
  matrix products  12.3 us (5%)
  local copies, waits for them, and re-layouts  8.09 us (3%)
  waiting for transfers between devices  2.87 us (1%)
    pallas_call x1, Pallas kernels, attention(): pl.pallas_call(functools.partial(attend_kernel, nb, nu), out_shape=jax.Sh...  75.5 us
    pallas_call x2, Pallas kernels, spread(): pl.pallas_call(functools.partial(spread_kernel, nb, nu, own_branch), out_...  60.3 us
    pallas_call x1, Pallas kernels, middle(): pl.pallas_call(functools.partial(middle_kernel, nu), out_shape=(jax.Shape...  30.6 us
    pallas_call x1, Pallas kernels, project(): pl.pallas_call(functools.partial(project_kernel, nu), out_shape=jax.Shape...  26.5 us
    pallas_call x1, Pallas kernels, last(): pl.pallas_call(functools.partial(last_kernel, nu), out_shape=jax.ShapeDty...  25.3 us
    dot_general x1, matrix products, body(): lax.dot_general(feed_hidden, reduce_full_t, (((1,), (1,)), ((), ())), pre...  11.5 us
  transfers between devices with their start and end apart: 2, of which 1 were waited for; matrix products, arithmetic and copies ran while one was open for 3% of the time, Pallas kernels for 75%

profile of v1, /device:TPU:33, one launch (start us, length us, event | category | flops | bytes accessed | tf_op | source)
XLA Modules:
  0.0 257.8 jit_solution(16997891734585669114)
XLA Ops:
  6.5 0.0 copy-start
  6.6 0.0 copy-start.5
  6.6 0.0 copy-start.3
  6.6 0.0 copy-start.1
  6.6 0.1 all-gather.3.cloned.1.call-start
  6.6 0.7 all-gather.3.cloned.1.call-update
  7.3 0.1 all-gather.5.cloned.1.call-start
  7.4 0.0 copy-start.4
  7.4 0.7 all-gather.5.cloned.1.call-update
  8.8 0.1 sine_convert_fusion
  8.9 0.0 copy-done
  8.9 0.3 convolution_reduce_fusion
  9.9 0.0 copy-done.5
  9.9 0.1 fusion.45
  10.0 0.6 fusion.37.part_ref
  10.6 39.9 %spread_0.1 = f32[16,8,1,128]{3,2,1,0:T(1,128)} custom-call(f32[1,1,128]{2,1,0:T(1,128)} %fusion.37.part_ref), custom_call_target="tpu_custom_call" | custom-call | tf_op jit(solution)/shard_map/spread_0/pallas_call | solution.py:126
  50.5 1.0 slice_reduce_fusion.1
  51.5 0.2 add.85
  51.8 0.0 copy-done.3
  51.8 0.0 copy-done.1
  51.8 0.3 fusion.14
  52.1 0.6 broadcast_in_dim.20.part_ref
  52.7 20.4 %spread_1.1 = f32[16,8,1,256]{3,2,1,0:T(1,128)} custom-call(f32[2,1,256]{2,1,0:T(1,128)} %broadcast_in_dim.20.part_ref), custom_call_target="tpu_custom_call" | custom-call | tf_op jit(solution)/shard_map/spread_1/pallas_call | solution.py:126
  73.1 1.2 slice_reduce_fusion
  74.4 0.9 reshape_squeeze.4.mod_ref
  75.3 0.0 copy-done.4
  75.3 0.7 tile.10.gain_ref
  76.0 26.5 %project.1.unit_ref = bf16[8,416,128]{2,1,0:T(8,128)(2,1)} custom-call(bf16[64,2432]{1,0:T(8,128)(2,1)} %bitcast.30, bf16[6,2432]{1,0:T(8,128)(2,1)} %bitcast.36, f32[10,2432]{1,0:T(8,128)} %reshape_squeeze.4.mod_ref, f32[3,256]{1,0:T(4,128)} %tile.10.gain_ref, bf16[5,2432,256]{2,1,0:T(8,128)(2,1)} %w_ref.1), custom_call_target="tpu_custom_call" | custom-call | tf_op jit(solution)/shard_map/project/pallas_call | solution.py:265
  102.5 0.8 slice_reduce_fusion.2
  103.4 0.7 and_select_fusion.bias_ref
  104.1 0.0 copy-start.2
  104.1 75.5 %attend.1.part = bf16[4,64,2432]{2,1,0:T(8,128)(2,1)} custom-call(bf16[8,416,128]{2,1,0:T(8,128)(2,1)} %project.1.unit_ref, f32[2,1,512]{2,1,0:T(1,128)} %and_select_fusion.bias_ref, bf16[256,2432]{1,0:T(8,128)(2,1)} %wo_ref.1), custom_call_target="tpu_custom_call" | custom-call | tf_op jit(solution)/shard_map/attend/pallas_call | solution.py:499
  179.5 30.6 %middle.1 = (bf16[8,64,2432]{2,1,0:T(8,128)(2,1)}, f32[64,2432]{1,0:T(8,128)}) custom-call(bf16[4,64,2432]{2,1,0:T(8,128)(2,1)} %attend.1.part, bf16[64,2432]{1,0:T(8,128)(2,1)} %bitcast.31, f32[10,2432]{1,0:T(8,128)} %reshape_squeeze.4.mod_ref), custom_call_target="tpu_custom_call" | custom-call | tf_op jit(solution)/shard_map/middle/pallas_call | solution.py:579
  210.2 0.0 copy-done.2
  210.2 0.9 pad.14.fw_ref
  211.1 0.0 all-gather.3.cloned.1.call-done
  211.1 1.4 all-gather.5.cloned.1.call-done
  212.5 11.5 %convolution_convert_fusion = bf16[512,2432]{1,0:T(8,128)(2,1)} fusion(bf16[2432,896]{1,0:T(8,128)(2,1)} %all-gather.5.cloned.1.call-done, bf16[512,2432]{1,0:T(8,128)(2,1)} %bitcast.37, bf16[2432,896]{1,0:T(8,128)(2,1)} %all-gather.3.cloned.1.call-done), kind=kOutput, calls=%fused_computation | convolution fusion | flops 4468113408 | bytes 13697024 | tf_op jit(solution)/shard_map/dot_general | solution.py:719
  224.0 25.3 %last.1 = f32[64,128]{1,0:T(8,128)} custom-call(bf16[2,4,64,2432]{3,2,1,0:T(8,128)(2,1)} %bitcast.29, f32[64,2432]{1,0:T(8,128)} %get-tuple-element.8.res_ref, f32[10,2432]{1,0:T(8,128)} %reshape_squeeze.4.mod_ref, bf16[128,2432]{1,0:T(8,128)(2,1)} %pad.14.fw_ref), custom_call_target="tpu_custom_call" | custom-call | tf_op jit(solution)/shard_map/last/pallas_call | solution.py:638
  249.3 0.8 constant_dynamic-slice_fusion
  250.1 0.1 copy.15
  250.2 0.1 copy.16
  250.3 0.7 copy.17
  (8 shorter events, 0.1 us)
Async XLA Ops:
  6.5 2.3 copy-start
  6.6 3.3 %copy-start.5 = (bf16[2432,19]{0,1:T(8,128)(2,1)S(1)}, bf16[2432,19]{0,1:T(8,128)(2,1)}, u32[]{:S(2)}) copy-start(bf16[2432,19]{0,1:T(8,128)(2,1)} %param.20) | copy-start | bytes 277252
  6.6 45.2 %copy-start.3 = (f32[2,1,2432]{2,1,0:T(1,128)S(1)}, f32[2,1,2432]{2,1,0:T(1,128)}, u32[]{:S(2)}) copy-start(f32[2,1,2432]{2,1,0:T(1,128)} %param.18) | copy-start | bytes 58372
  6.6 45.2 %copy-start.1 = (bf16[2432,190]{0,1:T(8,128)(2,1)S(1)}, bf16[2432,190]{0,1:T(8,128)(2,1)}, u32[]{:S(2)}) copy-start(bf16[2432,190]{0,1:T(8,128)(2,1)} %param.21) | copy-start | bytes 2772484
  6.6 204.5 %all-gather.3.cloned.1.call-start = ((), (), s32[]{:S(2)}) async-start(), calls=%async_computation | async-start | bytes 4630528 | tf_op jit(solution)/shard_map/all_gather | solution.py:684
  7.3 205.2 %all-gather.5.cloned.1.call-start = ((), (), s32[]{:S(2)}) async-start(), calls=%async_computation.1 | async-start | bytes 4630528 | tf_op jit(solution)/shard_map/all_gather | solution.py:685
  7.4 67.9 %copy-start.4 = (f32[3,64]{1,0:T(4,128)S(1)}, f32[3,64]{1,0:T(4,128)}, u32[]{:S(2)}) copy-start(f32[3,64]{1,0:T(4,128)} %param.26) | copy-start | bytes 2308
  104.1 106.1 %copy-start.2 = (bf16[2432,64]{0,1:T(8,128)(2,1)S(1)}, bf16[2432,64]{0,1:T(8,128)(2,1)}, u32[]{:S(2)}) copy-start(bf16[2432,64]{0,1:T(8,128)(2,1)} %param.27) | copy-start | bytes 933892
Sparse Core Ops, SparseCore 0:
  9.2 90.1 all-gather.2
  101.2 111.2 all-gather.4
